TPU v7x, 32 devices: a whole 2x2x4 slice. The times are simulated.
32 devices in a mesh: row: 8 (over z, x), col: 4 (over y, core).
Axes of the slice: x: 2, y: 2, z: 4, core: 2. Of those that a mesh axis runs over, the one named last changes fastest.
Arguments:
- factor_u: float32 [1, 8, 2, 4, 512, 128], P(None, 'row', None, 'col'), may hold values from -6 to 6
- factor_v: float32 [1, 8, 2, 4, 512, 128], P(None, 'row', None, 'col'), may hold values from -6 to 6
- near_field: float32 [2, 512, 512], replicated, as said below
- sketch: float32 [2, 512, 128], replicated, may hold values from -6 to 6
- tile_ranks: int32 [3, 1, 8, 2, 4], P(None, None, None, None, 'col'), may hold values from 1 to 128, as said below
Outputs:
- out_u: float32 [1, 8, 2, 4, 512, 128], P(None, 'row', None, 'col')
- out_v: float32 [1, 8, 2, 4, 512, 128], P(None, 'row', None, 'col')
Inputs may be any that keep to these rules, and one draw needn't show every extreme that they name: tile_ranks[0] is at least 16 and equals 128 on every tile (i, i); tile_ranks[1] lies between tile_ranks[0] - tile_ranks[0] // 2 and tile_ranks[0] - max(1, tile_ranks[0] // 4); tile_ranks[2] is at least 1 and at most tile_ranks[1], and when tile_ranks[1] > 1 it is at most tile_ranks[1] - max(1, tile_ranks[1] // 4). The diagonal entries of near_field[0] and near_field[1] lie between 1 and 4.
All inputs are finite; a program needn't handle non-finite values.
Results may differ from a plain program's by a relative error of at most 0.0003.
Values sent between devices are 32-bit elements; how exact they have to be, the bound alone decides.
A program may use at most 64 MiB of HBM per device.

v0:
```python
import functools
import math

import jax
import jax.numpy as jnp
from jax import lax
from jax.experimental import pallas as pl
from jax.experimental.pallas import tpu as pltpu
from jax.sharding import PartitionSpec as P

NS_STEPS = 3
BLOCK = 16
F32 = jnp.float32
BF16 = jnp.bfloat16
VMEM_SPEC = pl.BlockSpec(memory_space=pltpu.VMEM)
SMEM_SPEC = pl.BlockSpec(memory_space=pltpu.SMEM)
MESH = pl.DeviceIdType.MESH


def split(x):
    high = x.astype(BF16)
    return high, (x - high.astype(F32)).astype(BF16)


def dot_pairs(a, b, contract_b=0):
    dims = (((1,), (contract_b,)), ((), ()))
    ah, al = a
    bh, bl = b
    mm = lambda p, q: lax.dot_general(p, q, dims, preferred_element_type=F32)
    return mm(ah, bh) + (mm(ah, bl) + mm(al, bh))


def dot(a, b):
    return dot_pairs(split(a), split(b))


def dot_nt(a, b):
    return dot_pairs(split(a), split(b), 1)


def dot_tn(a, b):
    return dot_pairs(split(a.T), split(b))


def apply_inverse(matrix, scale, w):
    pair = split(matrix)

    def step(level, x):
        if level == 0:
            return scale * x
        y = step(level - 1, x)
        return step(level - 1, 2.0 * x - dot_pairs(pair, split(y)))

    return step(NS_STEPS, w)


def diagonal_inverse(near):
    n = near.shape[0]
    eye = lax.broadcasted_iota(jnp.int32, (n, n), 0) == lax.broadcasted_iota(jnp.int32, (n, n), 1)
    return 1.0 / jnp.sum(jnp.where(eye, near, 0.0), axis=1, keepdims=True)


def cholesky_inverse(grams, order):
    width = grams[0].shape[1]
    count = len(grams)
    eye = (
        lax.broadcasted_iota(jnp.int32, (order, width), 0) == lax.broadcasted_iota(jnp.int32, (order, width), 1)
    ).astype(F32)
    rest = [jnp.concatenate([g[:order], eye], axis=1) for g in grams]
    done = []
    start = 0
    while start < order:
        size = min(BLOCK, order - start)
        row_id = lax.broadcasted_iota(jnp.int32, (1, size, width), 1)
        rows = jnp.stack([x[:size] for x in rest])
        cols = jnp.stack(
            [
                jnp.stack([jnp.broadcast_to(x[:size, start + j : start + j + 1], (size, width)) for x in rest])
                for j in range(size)
            ]
        )
        scale = jnp.ones((count, size, width), F32)
        for k in range(size):
            lead = cols[0]
            inv = lax.rsqrt(lead[:, k : k + 1])
            m = jnp.where(row_id > k, lead * (inv * inv), 0.0)
            if k + 1 < size:
                cols = cols[1:]
                cols = cols - m[None] * cols[:, :, k : k + 1]
            rows = rows - jnp.concatenate([m, m], axis=2) * rows[:, k : k + 1]
            scale = jnp.where(row_id == k, inv, scale)
        rows = rows * jnp.concatenate([scale, scale], axis=2)
        done.append(rows[:, :, width:])
        end = start + size
        if end < order:
            rest = [
                rest[t][size:]
                - jnp.dot(
                    rows[t][:, :width].T[end:order],
                    rows[t],
                    precision=lax.Precision.HIGHEST,
                    preferred_element_type=F32,
                )
                for t in range(count)
            ]
        start = end
    if order < width:
        done.append(jnp.zeros((count, width - order, width), F32))
    inverses = jnp.concatenate(done, axis=1)
    return [inverses[t] for t in range(count)]


def orthonormal(bases, ranks, order):
    width = bases[0].shape[1]
    row = lax.broadcasted_iota(jnp.int32, (width, width), 0)
    col = lax.broadcasted_iota(jnp.int32, (width, width), 1)
    grams = []
    for basis, rank in zip(bases, ranks):
        gram = dot_tn(basis, basis)
        grams.append(gram + jnp.where((row == col) & (col >= rank), 1.0, 0.0))
    inverses = cholesky_inverse(grams, order)
    return [dot_nt(basis, inverse) for basis, inverse in zip(bases, inverses)]


def recompress(us, vs, wides, ups, sketch, ranks, order):
    height, width = us[0].shape
    root_order = math.sqrt(height)
    sk = split(sketch)
    bases = []
    for u, v, wide, up, rank in zip(us, vs, wides, ups, ranks):
        here = dot_pairs(split(v.T), sk)
        above = dot_pairs(split(up.T), sk)
        basis = dot(u, here) - dot(wide, above)
        keep = lax.broadcasted_iota(jnp.int32, (height, width), 1) < rank
        bases.append(jnp.where(keep, basis, 0.0))
    orthos = orthonormal(orthonormal(bases, ranks, order), ranks, order)
    out = []
    for u, v, wide, up, ortho in zip(us, vs, wides, ups, orthos):
        o = split(ortho)
        new_v = dot(v, dot_pairs(split(u.T), o)) - dot(up, dot_pairs(split(wide.T), o))
        out.append((ortho * root_order, new_v * (1.0 / root_order)))
    return out


class Tree:
    def __init__(self, root, edges):
        self.root = root
        self.edges = edges


def row_tree(n, source, r, c, direct=False):
    levels = n // 2
    level, side, e = r // 2, (r + source) % 2, c % 2
    index = lambda l, s: 2 * l + (s + source) % 2
    spine = side == e
    edges = [
        (spine & (level + 1 < levels), (index(level + 1, e), c)),
        ((level == 0) & (side == 0) if direct else jnp.logical_not(spine) & (level == 1 - e), (index(0, 1), c)),
        (spine & (level >= 1), (index(level, 1 - e), c)),
    ]
    return Tree((level == 0) & (side == 0), edges)


def col_tree(n, source, r, c):
    levels = n // 2
    level, side = c // 2, (c + source) % 2
    index = lambda l, s: 2 * l + (s + source) % 2
    edges = [
        ((side == 0) & (level + 1 < levels), (r, index(level + 1, 0))),
        (side == 0, (r, index(level, 1))),
    ]
    return Tree((level == 0) & (side == 0), edges)


class Piece:
    def __init__(self, tree, own, ref, send, recv, when=None):
        self.tree, self.own, self.ref, self.send, self.recv, self.when = tree, own, ref, send, recv, when

    def both(self, cond):
        return cond if self.when is None else cond & self.when

    def begin(self):
        @pl.when(self.both(self.tree.root))
        def _():
            pltpu.make_async_copy(self.own, self.ref, self.recv).start()

    def copy(self, k, device):
        return pltpu.make_async_remote_copy(
            src_ref=self.ref,
            dst_ref=self.ref,
            send_sem=self.send.at[min(k, 1)],
            recv_sem=self.recv,
            device_id=device,
            device_id_type=MESH,
        )

    def forward(self, only=None):
        both = lambda cond: self.both(cond if only is None else cond & only)

        def wait():
            pltpu.make_async_copy(self.ref, self.ref, self.recv).wait()

        if self.when is None and only is None:
            wait()
        else:
            pl.when(self.when if only is None else self.both(only))(wait)
        for k, (cond, device) in enumerate(self.tree.edges):
            @pl.when(both(cond))
            def _(k=k, device=device):
                self.copy(k, device).start()

    def finish(self):
        for k, (cond, device) in enumerate(self.tree.edges):
            @pl.when(self.both(cond))
            def _(k=k, device=device):
                self.copy(k, device).wait_send()


def greet_all(n_row, n_col, r, c):
    barrier = pltpu.get_barrier_semaphore()
    for d in range(1, n_row):
        pl.semaphore_signal(barrier, inc=1, device_id=((r + d) % n_row, c), device_id_type=MESH)
    for d in range(1, n_col):
        pl.semaphore_signal(barrier, inc=1, device_id=(r, (c + d) % n_col), device_id_type=MESH)
    pl.semaphore_wait(barrier, n_row + n_col - 2)


def parts(ref, lead, part, count=2):
    view = ref if lead is None else ref.at[lead]
    rows = view.shape[0] // count
    return view.at[pl.ds(part * rows, rows)]


def kernel(n_row, n_col, order_1, order_2, ranks, u, v, near, sketch, out_u, out_v, *scratch):
    (up_u, up_v, low_u, low_v, p_u, p_v, q, u1, v1, y, wide_own, up_y, up_v1, low_u1, low_v1, up_pivot, lower_1, send, recv) = scratch
    r, c = lax.axis_index("row"), lax.axis_index("col")
    far = 1.0 / (8.0 * u.shape[1])
    width = u.shape[2]
    greet_all(n_row, n_col, r, c)
    rt0, rt1 = row_tree(n_row, 0, r, c), row_tree(n_row, 1, r, c)
    rt0_first = row_tree(n_row, 0, r, c, True)
    ct0, ct1 = col_tree(n_col, 0, r, c), col_tree(n_col, 1, r, c)
    pieces = []

    def piece(tree, own, ref, when=None):
        k = len(pieces)
        pieces.append(Piece(tree, own, ref, send.at[k], recv.at[k], when))
        return pieces[-1]

    two = range(2)
    first_row = r == 1
    low = [piece(ct0, parts(a, 0, h), parts(b, None, h)) for h in two for a, b in ((u, low_u), (v, low_v))]
    chain = [
        piece(tree, parts(a, t, h), parts(b, t, h))
        for t, tree in ((0, rt0_first), (1, rt0))
        for a, b in ((u, up_u), (v, up_v))
        for h in two
    ]
    pivot = [piece(ct0, parts(a, 0, h), parts(b, None, h)) for a, b in ((up_u, p_u), (up_v, p_v)) for h in two]
    q_own = [piece(ct1, parts(a, 0, h), parts(q, k, h), first_row) for k, a in ((0, u), (1, v)) for h in two]
    q_up = [piece(ct1, parts(a, 0, h), parts(q, k, h), first_row) for k, a in ((2, up_u), (3, up_v)) for h in two]
    low1 = [piece(ct1, parts(a, 0, h), parts(b, None, h)) for h in two for a, b in ((u1, low_u1), (v1, low_v1))]
    chain_v = [
        piece(rt1, parts(v1, t, h), parts(up_v1, t, h), when) for t, when in ((0, c != 1), (1, None)) for h in two
    ]
    quarters = range(4)
    chain_y = [
        piece(rt1, parts(y, t, h, 4), parts(up_y, t, h, 4), when)
        for t, when in ((0, c != 1), (1, None))
        for h in quarters
    ]
    extra = [
        piece(rt1, parts(a, lead, h), parts(up_pivot, k, h), c == 1)
        for k, a, lead in ((0, wide_own, None), (1, u1, 0), (2, v1, 0))
        for h in two
    ]

    for x in chain + low + q_own:
        x.begin()
    for x in low:
        x.forward()
    for k in range(4):
        chain[k].forward()
        pivot[k].begin()
        q_up[k].begin()
    for k in range(4):
        chain[4 + k].forward()
        pivot[k].forward()
    for x in q_own + q_up:
        x.forward(c == 1)
    pivot_t = near[0].T + far * dot_nt(p_v[...], p_u[...])
    lower = apply_inverse(pivot_t, diagonal_inverse(near[0]), low_v[...])
    for x in q_own + q_up:
        x.forward(c != 1)
    lower_t = split(lower.T)
    lead = split(low_u[...])
    wide_of = lambda up: dot_pairs(lead, split(far * dot_pairs(lower_t, split(up))))
    us, vs = [u[t] for t in two], [v[t] for t in two]
    fresh = recompress(
        us, vs, [wide_of(up_u[t]) for t in two], [up_v[t] for t in two], sketch[0], [ranks[1, t] for t in two], order_1
    )
    for t in two:
        j = t * n_col + c
        chosen = (r > 0) & (j > 0) & jnp.logical_not((r == 1) & (j == 1))
        pivot_here = (r == 0) & (j == 0)
        lower_here = (r > 0) & (j == 0)
        u1[t] = jnp.where(pivot_here, 0.0, jnp.where(chosen, fresh[t][0], us[t]))
        v1[t] = jnp.where(pivot_here, 0.0, jnp.where(lower_here, lower, jnp.where(chosen, fresh[t][1], vs[t])))

    @pl.when(first_row)
    def _():
        wide_own[...] = wide_of(q[2])

    for x in low1 + extra + chain_v:
        x.begin()
    for x in low1 + extra:
        x.forward()
    for x in chain_v:
        x.forward(first_row)

    @pl.when((c == 1) & (r > 1))
    def _():
        pivot_1t = near[1].T + far * (dot_nt(up_pivot[2], up_pivot[1]) - dot_nt(up_v[0], up_pivot[0]))
        lower_1[...] = apply_inverse(pivot_1t, diagonal_inverse(near[1]), v1[0])

    for x in chain_v:
        x.forward(r != 1)

    @pl.when(first_row)
    def _():
        pivot_1 = near[1] + far * (dot_nt(q[0], q[1]) - dot_nt(wide_own[...], q[3]))
        applied = apply_inverse(pivot_1, diagonal_inverse(near[1]), jnp.concatenate([u1[0], u1[1]], axis=1))
        y[0] = applied[:, :width]
        y[1] = applied[:, width:]

    for x in chain_y:
        x.begin()
    for x in chain_y:
        x.forward()
    lower_t1 = split(low_v1[...].T)
    lead_1 = split(low_u1[...])
    us, vs = [u1[t] for t in two], [v1[t] for t in two]
    wides = [dot_pairs(lead_1, split(far * dot_pairs(lower_t1, split(up_y[t])))) for t in two]
    fresh = recompress(us, vs, wides, [up_v1[t] for t in two], sketch[1], [ranks[2, t] for t in two], order_2)
    for t in two:
        j = t * n_col + c
        chosen = (r > 1) & (j > 1)
        out_u[t] = jnp.where(chosen, fresh[t][0], us[t])
        out_v[t] = jnp.where(chosen, fresh[t][1], vs[t])

    @pl.when((c == 1) & (r > 1))
    def _():
        out_v[0] = lower_1[...]

    for x in pieces:
        x.finish()


def body(n_row, n_col, factor_u, factor_v, near_field, sketch, tile_ranks):
    tiles, height, width = factor_u.shape[2], factor_u.shape[4], factor_u.shape[5]
    row_here = lax.axis_index("row")
    ranks = lax.dynamic_slice_in_dim(tile_ranks, row_here, 1, 2).reshape(3, tiles)
    keep = (jnp.arange(width, dtype=jnp.int32) < ranks[0][:, None]).astype(F32)[:, None, :]
    u = factor_u.reshape(tiles, height, width) * keep
    v = factor_v.reshape(tiles, height, width) * keep
    pair, one = (tiles, height, width), (height, width)
    order_1 = width - max(1, width // 4)
    order_2 = order_1 - max(1, order_1 // 4)
    buffers = [pair, pair, one, one, one, one, (4, height, width), pair, pair, pair, one, pair, pair, one, one, (3, height, width), one]
    pieces = 46
    out_u, out_v = pl.pallas_call(
        functools.partial(kernel, n_row, n_col, order_1, order_2),
        out_shape=[jax.ShapeDtypeStruct(pair, F32)] * 2,
        in_specs=[SMEM_SPEC] + [VMEM_SPEC] * 4,
        out_specs=[VMEM_SPEC] * 2,
        scratch_shapes=[pltpu.VMEM(s, F32) for s in buffers]
        + [pltpu.SemaphoreType.DMA((pieces, 2)), pltpu.SemaphoreType.DMA((pieces,))],
        compiler_params=pltpu.CompilerParams(
            collective_id=0, has_side_effects=True, vmem_limit_bytes=60 * 1024 * 1024
        ),
    )(ranks, u, v, near_field, sketch)
    tile_col = jnp.arange(tiles, dtype=jnp.int32) * n_col + lax.axis_index("col")
    stays = jnp.logical_not((row_here == 1) & (tile_col == 1))[:, None, None]
    out_u, out_v = jnp.where(stays, out_u, 0.0), jnp.where(stays, out_v, 0.0)
    shape_out = (1, 1, tiles, 1, height, width)
    return (out_u.reshape(shape_out), out_v.reshape(shape_out))


def solution(mesh):
    return jax.shard_map(
        functools.partial(body, mesh.shape["row"], mesh.shape["col"]),
        mesh=mesh,
        in_specs=(
            P(None, "row", None, "col", None, None),
            P(None, "row", None, "col", None, None),
            P(),
            P(),
            P(None, None, None, None, "col"),
        ),
        out_specs=(
            P(None, "row", None, "col", None, None),
            P(None, "row", None, "col", None, None),
        ),
        check_vma=False,
    )
```

profile of v0, /device:TPU:28, one launch (start us, length us, event | category | flops | bytes accessed | tf_op | source)
XLA Modules:
  0.0 103.2 jit_solution(11666346599844697299)
XLA Ops:
  0.6 0.0 copy-start
  0.7 0.7 copy-done
  1.3 0.2 dynamic-slice_reduce_fusion
  1.5 0.1 compare_convert_fusion
  1.6 0.1 constant_dynamic-slice_fusion
  1.7 0.1 copy.11
  1.8 0.7 copy.12.ranks
  2.4 2.2 %bitcast_multiply_fusion = (f32[2,512,128]{2,1,0:T(8,128)}, f32[2,512,128]{2,1,0:T(8,128)}) fusion(f32[1,1,2,1,512,128]{5,4,3,2,1,0:T(8,128)} %param.6, f32[2,128]{1,0:T(2,128)S(1)} %compare_convert_fusion, f32[1,1,2,1,512,128]{5,4,3,2,1,0:T(8,128)} %param.5), kind=kLoop, calls=%fused_computation | loop fusion | flops 262144 | bytes 2098176 | tf_op jit(solution)/shard_map/mul | solution.py:365
  4.7 96.2 %shard_map.68 = (f32[2,512,128]{2,1,0:T(8,128)}, f32[2,512,128]{2,1,0:T(8,128)}) custom-call(s32[3,2]{1,0:T(4,128)} %copy.12.ranks, f32[2,512,128]{2,1,0:T(8,128)} %get-tuple-element.11.u, f32[2,512,128]{2,1,0:T(8,128)} %get-tuple-element.10.v, f32[2,512,512]{2,1,0:T(8,128)} %near.1, f32[2,512,128]{2,1,0:T(8,128)} %sketch.1), custom_call_target="tpu_custom_call" | custom-call | tf_op jit(solution)/shard_map/pallas_call | solution.py:371
  100.9 2.3 %select_bitcast_fusion = (f32[1,1,2,1,512,128]{5,4,3,2,1,0:T(8,128)}, f32[1,1,2,1,512,128]{5,4,3,2,1,0:T(8,128)}) fusion(f32[2,512,128]{2,1,0:T(8,128)} %get-tuple-element.5, pred[2]{0:T(512)(128)(4,1)S(1)} %and_not_fusion, f32[2,512,128]{2,1,0:T(8,128)} %get-tuple-element.4), kind=kLoop, calls=%fused_computation.2 | loop fusion | flops 262144 | bytes 2097154
  (1 shorter events, 0.0 us)
Async XLA Ops:
  0.6 0.7 copy-start
where the time goes:
time: 103 us
  Pallas kernels  96.2 us (93%)
  other arithmetic  4.62 us (4%)
  local copies, waits for them, and re-layouts  1.69 us (2%)
    pallas_call x1, Pallas kernels, body(): pl.pallas_call(functools.partial(kernel, n_row, n_col, order_1, order_2),...  96.2 us
    unnamed x1, other arithmetic  2.3 us
    mul x1, other arithmetic, body(): v = factor_v.reshape(tiles, height, width) * keep  2.24 us

commit v1 on v0

v1 whole, which is shorter than its diff:
```python
import functools
import math

import jax
import jax.numpy as jnp
from jax import lax
from jax.experimental import pallas as pl
from jax.experimental.pallas import tpu as pltpu
from jax.sharding import PartitionSpec as P

NS_STEPS = 3
BLOCK = 16
EDGES = 5
F32 = jnp.float32
BF16 = jnp.bfloat16
MESH = pl.DeviceIdType.MESH


def split(x):
    high = x.astype(BF16)
    return high, (x - high.astype(F32)).astype(BF16)


def mm(a, b, contract_b=0):
    return lax.dot_general(a, b, (((1,), (contract_b,)), ((), ())), preferred_element_type=F32)


def stacked(a, b, contract_b=0):
    ah, al = a
    bh, bl = b
    n = ah.shape[0]
    both = mm(jnp.concatenate([ah, al], axis=0), bh, contract_b)
    return both[:n] + both[n:] + mm(ah, bl, contract_b)


def deep(a, b, contract_b=0):
    ah, al = a
    bh, bl = b
    axis = contract_b
    return mm(jnp.concatenate([ah, al], axis=1), jnp.concatenate([bh, bh], axis=axis), contract_b) + mm(
        ah, bl, contract_b
    )


def pad_rows(x, n):
    if x.shape[0] == n:
        return x
    return jnp.concatenate([x, jnp.zeros((n - x.shape[0], x.shape[1]), x.dtype)], axis=0)


def apply_inverse(high, low, scale, w, hooks):
    n = w.shape[1]
    x = scale * w
    for step in range(2**NS_STEPS - 1):
        xh, xl = split(x)
        both = mm(high[...], jnp.concatenate([xh, xl], axis=1))
        x = x + scale * (w - (both[:, :n] + both[:, n:] + mm(low[...], xh)))
        if step in hooks:
            hooks[step]()
    return x


def diagonal_inverse(near):
    n = near.shape[0]
    eye = lax.broadcasted_iota(jnp.int32, (n, n), 0) == lax.broadcasted_iota(jnp.int32, (n, n), 1)
    return 1.0 / jnp.sum(jnp.where(eye, near, 0.0), axis=1, keepdims=True)


def spread(x, j):
    return jnp.broadcast_to(x[:, j : j + 1], x.shape)


def whiten(grams, rights, order):
    count, width = len(grams), grams[0].shape[1]
    total = grams[0].shape[0]
    rest = [jnp.concatenate([g, x], axis=1) for g, x in zip(grams, rights)]
    done = [[] for _ in grams]
    start = 0
    while start < order:
        size = min(BLOCK, order - start)
        end = start + size
        tiles = size // 8
        row_id = lax.broadcasted_iota(jnp.int32, (1, 8, width), 1)
        column = lambda x, h, j: jnp.broadcast_to(x[8 * h : 8 * h + 8, start + j : start + j + 1], (8, width))
        cols = [
            [None if h < j // 8 else jnp.stack([column(x, h, j) for x in rest]) for h in range(tiles)]
            for j in range(size)
        ]
        rows = [jnp.stack([x[8 * h : 8 * h + 8] for x in rest]) for h in range(tiles)]
        lanes = rows[0].shape[2] // width
        along = lambda m: jnp.concatenate([m] * lanes, axis=2)
        scale = [jnp.ones((count, 8, width), F32) for _ in range(tiles)]
        for k in range(size):
            hk, rk = k // 8, k % 8
            lead = cols[k]
            inv = lax.rsqrt(spread(lead[hk], rk))
            inv2 = inv * inv
            masked = list(lead)
            masked[hk] = jnp.where(row_id > rk, lead[hk], 0.0)
            m = [None if x is None else x * inv2 for x in masked]
            for j in range(k + 1, size):
                hj, rj = j // 8, j % 8
                x = spread(lead[hj], rj)
                for h in range(hj, tiles):
                    step = (masked[h] * x) * inv2 if j == k + 1 else m[h] * x
                    cols[j][h] = cols[j][h] - step
            top = rows[hk][:, rk : rk + 1]
            for h in range(hk, tiles):
                rows[h] = rows[h] - along(m[h]) * top
            scale[hk] = jnp.where(row_id == rk, inv, scale[hk])
        rows = [x * along(s) for x, s in zip(rows, scale)]
        block = jnp.concatenate(rows, axis=1) if tiles > 1 else rows[0]
        for t in range(count):
            done[t].append(block[t][:, width:])
        if end < order:
            new = []
            for t in range(count):
                high = block[t].astype(BF16).astype(F32)
                low = block[t] - high
                left = [high[:, :width], low[:, :width], high[:, :width]]
                left = jnp.concatenate(left, axis=0).T[end:order].astype(BF16)
                right = jnp.concatenate([high, high, low], axis=0).astype(BF16)
                new.append(rest[t][size : order - start] - mm(left, right))
            rest = new
        start = end
    return [pad_rows(jnp.concatenate(d, axis=0), total) for d in done]


def orthonormal(bases, ranks, order, width):
    count = bases[0].shape[0]
    row = lax.broadcasted_iota(jnp.int32, (count, width), 0)
    col = lax.broadcasted_iota(jnp.int32, (count, width), 1)
    grams = []
    for basis, rank in zip(bases, ranks):
        high, low = split(basis)
        gram = stacked((high, low), (pad_rows(high, width), pad_rows(low, width)), 1)
        grams.append(gram + jnp.where((row == col) & (col >= rank), 1.0, 0.0))
    return whiten(grams, bases, order)


def basis_of(here, above, u, wide, rank):
    rows = here.shape[0]
    keep = lax.broadcasted_iota(jnp.int32, (rows, 2 * here.shape[1]), 0) < rank
    both = jnp.where(keep, jnp.concatenate([here, -above], axis=1), 0.0)
    return stacked(split(both), split(jnp.concatenate([u, wide], axis=1)), 1)


def backward(ortho, u, wide):
    back = stacked(split(ortho), split(jnp.concatenate([u, wide], axis=1)))
    width = u.shape[1]
    return jnp.concatenate([back[:, :width], -back[:, width:]], axis=1)


def new_right(back, v, up):
    width = v.shape[1]
    bh, bl = split(back)
    bh, bl = pad_rows(bh, width), pad_rows(bl, width)
    vh, vl = split(jnp.concatenate([v, up], axis=1))
    both = mm(vh, jnp.concatenate([bh, bl], axis=0), 1)
    return both[:, :width] + both[:, width:] + mm(vl, bh, 1)


class Piece:
    def __init__(self, own, ref, root, has, edges, send, recv, local=False):
        self.own, self.ref, self.root, self.has, self.edges = own, ref, root, has, edges
        self.send, self.recv, self.local = send, recv, local

    def copy(self, k, src):
        return pltpu.make_async_remote_copy(
            src_ref=src,
            dst_ref=self.ref,
            send_sem=self.send.at[k],
            recv_sem=self.recv,
            device_id=self.edges[k][1],
            device_id_type=MESH,
        )

    def send_all(self, src):
        for k, (cond, _) in enumerate(self.edges):
            @pl.when(cond)
            def _(k=k):
                self.copy(k, src).start()

    def begin(self):
        @pl.when(self.root)
        def _():
            self.send_all(self.own)
            if self.local:
                pltpu.make_async_copy(self.own, self.ref, self.recv).start()

    def forward(self, only=None):
        both = lambda cond: cond if only is None else cond & only
        if self.local:
            @pl.when(both(self.root))
            def _():
                pltpu.make_async_copy(self.ref, self.ref, self.recv).wait()

        @pl.when(both(self.has))
        def _():
            pltpu.make_async_copy(self.ref, self.ref, self.recv).wait()
            self.send_all(self.ref)

    def finish(self):
        @pl.when(self.root | self.has)
        def _():
            for k, (cond, _) in enumerate(self.edges):
                @pl.when(cond)
                def _(k=k):
                    self.copy(k, self.ref).wait_send()


def greet_all(n_row, n_col, r, c):
    barrier = pltpu.get_barrier_semaphore()
    for d in range(1, n_row):
        pl.semaphore_signal(barrier, inc=1, device_id=((r + d) % n_row, c), device_id_type=MESH)
    for d in range(1, n_col):
        pl.semaphore_signal(barrier, inc=1, device_id=(r, (c + d) % n_col), device_id_type=MESH)
    pl.semaphore_wait(barrier, n_row + n_col - 2)


def part(ref, lead, k, count):
    view = ref if lead is None else ref.at[lead]
    rows = view.shape[0] // count
    return view.at[pl.ds(k * rows, rows)]


def kernel(n_row, n_col, order_1, order_2, ranks, hu, hv, hnear, hsketch, out_u, out_v, *scratch):
    (
        u, v, near, sk, near_t, high, low, p_u, p_v, low_u, low_v, up_u, up_v, above_own, above,
        ex_u, ex_v, ex_w, wide, lower, u1, v1, u1t_own, above1_own, up1t, up1_v, above1,
        low1_u, low1_own, low1_t, send, recv, load,
    ) = scratch
    r, c = lax.axis_index("row"), lax.axis_index("col")
    height, width = u.shape[1:]
    far = 1.0 / (8.0 * height)
    rows_1, rows_2 = above.shape[1], above1.shape[1]
    two = range(2)
    level, side, levels = r // 2, r % 2, n_row // 2
    parity = c % 2
    pieces = []

    def piece(own, ref, root, has, edges, local=False):
        k = len(pieces)
        pieces.append(Piece(own, ref, root, has, edges, send.at[k], recv.at[k], local))
        return pieces[-1]

    other_row, other_col = r + 1 - 2 * side, c + 1 - 2 * parity
    spine = side == parity
    down_on = spine & (level + 1 < levels), (r + 2, c)
    down_over = spine & (level >= 1), (other_row, c)
    down_first = r == 0, (1, c)
    if levels > 1:
        beside = [
            ((r == 0) & (parity == 1), (1, c)),
            ((parity == 0) & (level == 1) & (side == 1), (r - 2, c)),
        ]
    else:
        beside = [down_first]

    def only(cond, edges):
        return [(a & cond, d) for a, d in edges]

    def down(own, ref, when):
        return piece(own, ref, (r == 0) & when, (r > 0) & when, only(when, [down_on, down_over] + beside))

    def down_1(own, ref, on, when):
        at = side == on
        edges = [
            ((r == 1) & (on == 0), (0, c)),
            (at & (level + 1 < levels), (r + 2, c)),
            (at & (level >= 1), (other_row, c)),
        ]
        return piece(own, ref, (r == 1) & when, ((r > 1) | ((r == 0) & (on == 0))) & when, only(when, edges))

    def across(own, ref, source, when):
        at = parity == source % 2
        edges = [(at, (r, other_col)), (at & (c // 2 + 1 < n_col // 2), (r, c + 2))]
        return piece(own, ref, (c == source) & when, (c != source) & when, only(when, edges), True)

    def pivot(own, ref, k):
        mine = parity == k
        edges = only(mine, [down_first, ((r == 0) & (c + 2 < n_col), (0, c + 2)), down_on, down_over])
        edges.append((mine & (r > 0), (r, other_col)))
        root = (r == 0) & (c == 0)
        if k == 1:
            edges[1] = edges[1][0] | root, (0, jnp.where(root, 1, c + 2))
            edges[0] = edges[0][0] & jnp.logical_not(root), edges[0][1]
        has = jnp.where(mine, jnp.logical_not(root), r > 0)
        return piece(own, ref, root, has, edges)

    quarters, later_rows, always = range(4), r > 1, r >= 0
    pivots = [[pivot(part(a, 0, h, 4), part(b, None, h, 4), k) for h in quarters] for k, a, b in ((0, u, p_u), (1, v, p_v))]
    lows_v = [across(part(v, 0, h, 2), part(low_v, None, h, 2), 0, r > 0) for h in two]
    lows_u = [across(part(u, 0, h, 2), part(low_u, None, h, 2), 0, r > 0) for h in two]
    ups_u = [[down(part(u, t, h, 4), part(up_u, t, h, 4), c > 0 if t == 0 else always) for h in quarters] for t in two]
    ups_a = [down(above_own, above, always)]
    ups_v = [down(part(v, t, h, 2), part(up_v, t, h, 2), c > 0 if t == 0 else always) for t in two for h in two]
    extras = [down_1(a, b, 0, c == 1) for a, b in ((u.at[0], ex_u), (v.at[0], ex_v))]
    extra_w = [down_1(wide.at[0], ex_w, 0, c == 1)]
    chains_u = [
        down_1(part(u1t_own, t, h, 4), up1t.at[t].at[pl.ds(h * (rows_1 // 4), rows_1 // 4)], parity, c > 1 if t == 0 else always)
        for t in two
        for h in quarters
    ]
    chains_a = [down_1(above1_own, above1, parity, always)]
    chains_v = [down_1(part(v1, t, h, 2), part(up1_v, t, h, 2), parity, c > 1 if t == 0 else always) for t in two for h in two]
    lows1_u = [across(part(u1, 0, h, 2), part(low1_u, None, h, 2), 1, later_rows) for h in two]
    lows1_t = [across(part(low1_own, None, h, 2), part(low1_t, None, h, 2), 1, later_rows) for h in two]

    def begin(*groups):
        for g in groups:
            for x in g:
                x.begin()

    def forward(*groups, only=None):
        for g in groups:
            for x in g:
                x.forward(only)

    loads = [(hu, u), (hv, v), (hsketch, sk), (hnear, near)]
    copies = [pltpu.make_async_copy(a, b, load.at[k]) for k, (a, b) in enumerate(loads)]
    for x in copies:
        x.start()
    greet_all(n_row, n_col, r, c)
    for x in copies[:3]:
        x.wait()
    col_id = lax.broadcasted_iota(jnp.int32, (height, width), 1)
    for t in two:
        keep = col_id < ranks[0, 0, t, 0, r]
        u[t] = jnp.where(keep, u[t], 0.0)
        v[t] = jnp.where(keep, v[t], 0.0)
    begin(pivots[1], pivots[0], lows_v, lows_u, extras)
    sketch_t = [split(sk[k].T[:rows]) for k, rows in ((0, rows_1), (1, rows_2))]

    def here_of(v, k):
        both = stacked(sketch_t[k], split(jnp.concatenate([v[0], v[1]], axis=1)))
        return both[:, :width], both[:, width:]

    @pl.when(r == 0)
    def _():
        forward(pivots[0], pivots[1])
        begin(ups_u[0], ups_u[1])
        a, b = here_of(v, 0)
        above_own[0] = a
        above_own[1] = b
        begin(ups_a, ups_v)
        copies[3].wait()
        for t in two:
            stays = (c > 0) | (t > 0)
            out_u[t] = jnp.where(stays, u[t], 0.0)
            out_v[t] = jnp.where(stays, v[t], 0.0)
        forward(extras, extra_w, chains_u, chains_a, chains_v)

    @pl.when((r > 0) & (c == 0))
    def _():
        up_u[0] = jnp.zeros((height, width), F32)
        up_v[0] = jnp.zeros((height, width), F32)

    @pl.when(r > 0)
    def _():
        for t in two:
            up1t[t, rows_1:] = jnp.zeros((width - rows_1, height), F32)

        @pl.when(c < 2)
        def _():
            up1t[0, :rows_1] = jnp.zeros((rows_1, height), F32)
            up1_v[0] = jnp.zeros((height, width), F32)

        copies[3].wait()
        near_t[0] = near[0].T

        @pl.when((c == 1) & later_rows)
        def _():
            near_t[1] = near[1].T

        scale = diagonal_inverse(near[0])
        here = here_of(v, 0)
        for k in two:
            forward(pivots[k], only=parity == k)
        forward(extras, only=later_rows & (side == 0))
        forward(ups_u[0], ups_u[1], only=later_rows)
        forward(lows_v, lows_u)
        for k in two:
            forward(pivots[k], only=parity != k)
        pivot_t = near_t[0] + far * deep(split(p_v[...]), split(p_u[...]), 1)
        high[...], low[...] = split(pivot_t)
        ups = ups_u[0] + ups_u[1]
        hooks = {k: lambda k=k: forward(ups[k : k + 1], only=(r == 1) & (parity == 1)) for k in range(7)}
        hooks[7] = lambda: forward(ups[7:], only=(r == 1) & (parity == 1))
        lower[...] = apply_inverse(high, low, scale, low_v[...], hooks)
        hooks[7]()
        forward(ups, only=(r == 1) & (parity == 0))
        forward(extras, only=later_rows & (side == 1))
        forward(ups_a, ups_v[:1])
        core = far * stacked(
            split(lower[...].T), split(jnp.concatenate([up_u[0], up_u[1]], axis=1))
        )
        lane = lax.broadcasted_iota(jnp.int32, core.shape, 1)
        live = (lane < ranks[0, 0, 0, 0, 0]) | ((lane >= width) & (lane < width + ranks[0, 0, 1, 0, 0]))
        core = jnp.where(live, core, 0.0)
        both = deep(split(low_u[...]), split(core))
        wide[0] = both[:, :width]
        wide[1] = both[:, width:]
        begin(extra_w)
        forward(ups_v[1:2])
        rank_1 = [ranks[1, 0, t, 0, r] for t in two]
        bases = [basis_of(here[t], above[t], u[t], wide[t], rank_1[t]) for t in two]
        bases = orthonormal(bases, rank_1, order_1, width)
        forward(ups_v[2:])
        forward(extra_w, only=later_rows)
        orthos = orthonormal(bases, rank_1, order_1, width)
        root_order = math.sqrt(height)
        tile_col = [t * n_col + c for t in two]
        chosen = [(tile_col[t] > 0) & jnp.logical_not((r == 1) & (tile_col[t] == 1)) for t in two]
        for t in two:
            u1t_own[t] = orthos[t] * root_order
        begin(chains_u)
        for t in two:
            u1[t] = jnp.where(chosen[t], pad_rows(orthos[t] * root_order, width).T, u[t])
        begin(lows1_u)
        for t in two:
            right = new_right(backward(orthos[t], u[t], wide[t]), v[t], up_v[t]) * (1.0 / root_order)
            v1[t] = jnp.where(chosen[t], right, jnp.where(tile_col[t] == 0, lower[...], v[t]))
        here = here_of(v1, 1)
        above1_own[0] = here[0]
        above1_own[1] = here[1]
        begin(chains_a, chains_v)

        @pl.when(r == 1)
        def _():
            for t in two:
                stays = tile_col[t] != 1
                out_u[t] = jnp.where(stays, u1[t], 0.0)
                out_v[t] = jnp.where(stays, v1[t], 0.0)

        @pl.when(later_rows)
        def _():
            @pl.when(c == 1)
            def _():
                left = jnp.concatenate([ex_v[...], up_v[0]], axis=1)
                right = jnp.concatenate([ex_u[...], -ex_w[...]], axis=1)
                lh, ll = split(left)
                rh, rl = split(right)
                pivot_t = near_t[1] + far * (mm(lh, rh, 1) + (mm(lh, rl, 1) + mm(ll, rh, 1)))
                high[...], low[...] = split(pivot_t)
                lower[...] = apply_inverse(high, low, diagonal_inverse(near[1]), v1[0], {})
                low1_own[...] = lower[...].T[:rows_1]

            begin(lows1_t)
            forward(chains_u, lows1_u, chains_a, lows1_t)
            core = far * stacked(split(low1_t[...]), split(up1t[...].reshape(2 * width, height)), 1)
            both = deep(split(low1_u[...]), split(pad_rows(core, width)))
            wide[0] = both[:, :width]
            wide[1] = both[:, width:]
            rank_2 = [ranks[2, 0, t, 0, r] for t in two]
            bases = [basis_of(here[t], above1[t], u1[t], wide[t], rank_2[t]) for t in two]
            bases = orthonormal(bases, rank_2, order_2, width)
            forward(chains_v[:2])
            orthos = orthonormal(bases, rank_2, order_2, width)
            forward(chains_v[2:])
            for t in two:
                live = tile_col[t] > 1
                right = new_right(backward(orthos[t], u1[t], wide[t]), v1[t], up1_v[t]) * (1.0 / root_order)
                out_u[t] = jnp.where(live, pad_rows(orthos[t] * root_order, width).T, u1[t])
                out_v[t] = jnp.where(live, right, jnp.where(tile_col[t] == 1, lower[...], v1[t]))

    for x in pieces:
        x.finish()


def body(n_row, n_col, factor_u, factor_v, near_field, sketch, tile_ranks):
    tiles, height, width = factor_u.shape[2], factor_u.shape[4], factor_u.shape[5]
    u = factor_u.reshape(tiles, height, width)
    v = factor_v.reshape(tiles, height, width)
    ranks = jnp.transpose(tile_ranks, (0, 1, 3, 4, 2))
    pair, one = (tiles, height, width), (height, width)
    order_1 = width - max(1, width // 4)
    order_2 = order_1 - max(1, order_1 // 4)
    rows_1, rows_2 = -(-order_1 // 16) * 16, -(-order_2 // 16) * 16
    square = (height, height)
    f32 = lambda *shape: pltpu.VMEM(shape, F32)
    buffers = [f32(*s) for s in (pair, pair, (2,) + square, (2,) + one, (2,) + square)]
    buffers += [pltpu.VMEM(square, BF16)] * 2
    buffers += [f32(*s) for s in (one, one, one, one, pair, pair, (2, rows_1, width), (2, rows_1, width))]
    buffers += [f32(*s) for s in (one, one, one, pair, one, pair, pair, (2, rows_1, height), (2, rows_2, width))]
    buffers += [f32(*s) for s in ((2, width, height), pair, (2, rows_2, width), one, (rows_1, height), (rows_1, height))]
    pieces = 45
    any_spec = pl.BlockSpec(memory_space=pl.ANY)
    out_u, out_v = pl.pallas_call(
        functools.partial(kernel, n_row, n_col, order_1, order_2),
        out_shape=[jax.ShapeDtypeStruct(pair, F32)] * 2,
        in_specs=[pl.BlockSpec(memory_space=pltpu.SMEM)] + [any_spec] * 4,
        out_specs=[pl.BlockSpec(memory_space=pltpu.VMEM)] * 2,
        scratch_shapes=buffers
        + [
            pltpu.SemaphoreType.DMA((pieces, EDGES)),
            pltpu.SemaphoreType.DMA((pieces,)),
            pltpu.SemaphoreType.DMA((4,)),
        ],
        compiler_params=pltpu.CompilerParams(
            collective_id=0, has_side_effects=True, vmem_limit_bytes=60 * 1024 * 1024
        ),
    )(ranks, u, v, near_field, sketch)
    shape_out = (1, 1, tiles, 1, height, width)
    return (out_u.reshape(shape_out), out_v.reshape(shape_out))


def solution(mesh):
    tile_spec = P(None, "row", None, "col", None, None)
    return jax.shard_map(
        functools.partial(body, mesh.shape["row"], mesh.shape["col"]),
        mesh=mesh,
        in_specs=(tile_spec, tile_spec, P(), P(), P(None, None, None, None, "col")),
        out_specs=(tile_spec, tile_spec),
        check_vma=False,
    )
```

time: 103 us -> 89.4 us (0.87)
  the two profiles are of different devices: /device:TPU:28 before, /device:TPU:30 now
where the time goes in v1:
time: 89.4 us; the launch traced here: 89.1 us
  Pallas kernels  84.8 us (95%)
  local copies, waits for them, and re-layouts  3.74 us (4%)
    pallas_call x1, Pallas kernels, body(): pl.pallas_call(functools.partial(kernel, n_row, n_col, order_1, order_2),...  84.8 us
    unnamed x2, local copies, waits for them, and re-layouts  3.74 us

profile of v1, /device:TPU:30, one launch (start us, length us, event | category | flops | bytes accessed | tf_op | source)
XLA Modules:
  0.0 89.1 jit_solution(15047254134518190466)
XLA Ops:
  0.6 84.8 %shard_map.68 = (f32[2,512,128]{2,1,0:T(8,128)}, f32[2,512,128]{2,1,0:T(8,128)}) custom-call(s32[3,1,2,1,8]{4,3,2,1,0:T(1,128)} %bitcast.13, f32[2,512,128]{2,1,0:T(8,128)} %bitcast.11, f32[2,512,128]{2,1,0:T(8,128)} %bitcast.12, f32[2,512,512]{2,1,0:T(8,128)} %hnear.1, f32[2,512,128]{2,1,0:T(8,128)} %hsketch.1), custom_call_target="tpu_custom_call" | custom-call | tf_op jit(solution)/shard_map/pallas_call | solution.py:489
  85.4 1.9 %copy.11 = f32[1,1,2,1,512,128]{5,4,3,2,1,0:T(8,128)} copy(f32[1,1,2,1,512,128]{5,4,3,2,1,0:T(8,128)} %bitcast.10) | data formatting | bytes 1048576
  87.3 1.9 %copy.12 = f32[1,1,2,1,512,128]{5,4,3,2,1,0:T(8,128)} copy(f32[1,1,2,1,512,128]{5,4,3,2,1,0:T(8,128)} %bitcast.9) | data formatting | bytes 1048576

commit v2 on v1

--- a/solution.py
+++ b/solution.py
@@ -181,8 +181,8 @@
             def _(k=k):
                 self.copy(k, src).start()
 
-    def begin(self):
-        @pl.when(self.root)
+    def begin(self, only=None):
+        @pl.when(self.root if only is None else self.root & only)
         def _():
             self.send_all(self.own)
             if self.local:
@@ -260,8 +260,8 @@
     def only(cond, edges):
         return [(a & cond, d) for a, d in edges]
 
-    def down(own, ref, when):
-        return piece(own, ref, (r == 0) & when, (r > 0) & when, only(when, [down_on, down_over] + beside))
+    def down(own, ref, when, first):
+        return piece(own, ref, (r == 0) & when, (r > 0) & when, only(when, [down_on, down_over] + first))
 
     def down_1(own, ref, on, when):
         at = side == on
@@ -292,11 +292,11 @@
     pivots = [[pivot(part(a, 0, h, 4), part(b, None, h, 4), k) for h in quarters] for k, a, b in ((0, u, p_u), (1, v, p_v))]
     lows_v = [across(part(v, 0, h, 2), part(low_v, None, h, 2), 0, r > 0) for h in two]
     lows_u = [across(part(u, 0, h, 2), part(low_u, None, h, 2), 0, r > 0) for h in two]
-    ups_u = [[down(part(u, t, h, 4), part(up_u, t, h, 4), c > 0 if t == 0 else always) for h in quarters] for t in two]
-    ups_a = [down(above_own, above, always)]
-    ups_v = [down(part(v, t, h, 2), part(up_v, t, h, 2), c > 0 if t == 0 else always) for t in two for h in two]
-    extras = [down_1(a, b, 0, c == 1) for a, b in ((u.at[0], ex_u), (v.at[0], ex_v))]
-    extra_w = [down_1(wide.at[0], ex_w, 0, c == 1)]
+    ups_u = [[down(part(u, t, h, 4), part(up_u, t, h, 4), c > 0 if t == 0 else always, beside if t else [down_first]) for h in quarters] for t in two]
+    ups_a = [down(above_own, above, always, [down_first])]
+    ups_v = [down(part(v, t, h, 4), part(up_v, t, h, 4), c > 0 if t == 0 else always, beside) for t in two for h in quarters]
+    extras = [down_1(part(a, 0, h, 4), part(b, None, h, 4), 0, c == 1) for a, b in ((u, ex_u), (v, ex_v)) for h in quarters]
+    extra_w = [down_1(part(wide, 0, h, 4), part(ex_w, None, h, 4), 0, c == 1) for h in quarters]
     chains_u = [
         down_1(part(u1t_own, t, h, 4), up1t.at[t].at[pl.ds(h * (rows_1 // 4), rows_1 // 4)], parity, c > 1 if t == 0 else always)
         for t in two
@@ -307,10 +307,10 @@
     lows1_u = [across(part(u1, 0, h, 2), part(low1_u, None, h, 2), 1, later_rows) for h in two]
     lows1_t = [across(part(low1_own, None, h, 2), part(low1_t, None, h, 2), 1, later_rows) for h in two]
 
-    def begin(*groups):
+    def begin(*groups, only=None):
         for g in groups:
             for x in g:
-                x.begin()
+                x.begin(only)
 
     def forward(*groups, only=None):
         for g in groups:
@@ -338,8 +338,11 @@
 
     @pl.when(r == 0)
     def _():
+        for t in two:
+            begin(ups_u[t], only=parity != t)
         forward(pivots[0], pivots[1])
-        begin(ups_u[0], ups_u[1])
+        for t in two:
+            begin(ups_u[t], only=parity == t)
         a, b = here_of(v, 0)
         above_own[0] = a
         above_own[1] = b
@@ -375,23 +378,42 @@
 
         scale = diagonal_inverse(near[0])
         here = here_of(v, 0)
+        last = level + 1 == levels
+        relays = later_rows & jnp.logical_not(last) & (spine | ((level == 1) & (parity == 0)))
+        ends = later_rows & jnp.logical_not(relays)
+        middle = ((r == 1) & (parity == 1)) | (last & spine)
+        passes = relays | ((r == 1) & (parity == 1))
+        leads = lambda cond: [forward(ups_u[t], only=passes & (parity != t) & cond) for t in two]
+        forward(extras, only=later_rows & (side == 0))
+        leads(c >= 2)
         for k in two:
             forward(pivots[k], only=parity == k)
-        forward(extras, only=later_rows & (side == 0))
-        forward(ups_u[0], ups_u[1], only=later_rows)
+        leads(c < 2)
+        for t in two:
+            forward(ups_u[t], only=relays & (parity == t))
+        forward(ups_a, only=relays)
+        early = relays & (level == 1) & (parity == 0)
+        forward(ups_v, only=early)
         forward(lows_v, lows_u)
         for k in two:
             forward(pivots[k], only=parity != k)
         pivot_t = near_t[0] + far * deep(split(p_v[...]), split(p_u[...]), 1)
         high[...], low[...] = split(pivot_t)
-        ups = ups_u[0] + ups_u[1]
-        hooks = {k: lambda k=k: forward(ups[k : k + 1], only=(r == 1) & (parity == 1)) for k in range(7)}
-        hooks[7] = lambda: forward(ups[7:], only=(r == 1) & (parity == 1))
+        def hook(k):
+            for t in two:
+                if k < 4:
+                    forward(ups_u[t][k : k + 1], only=ends & (parity != t))
+                else:
+                    forward(ups_u[t][k - 4 : k - 3], only=(ends | ((r == 1) & (parity == 1))) & (parity == t))
+
+        hooks = {k: functools.partial(hook, k) for k in range(7)}
         lower[...] = apply_inverse(high, low, scale, low_v[...], hooks)
-        hooks[7]()
-        forward(ups, only=(r == 1) & (parity == 0))
+        hook(7)
+        forward(ups_u[1], ups_u[0], only=(r == 1) & (parity == 0))
         forward(extras, only=later_rows & (side == 1))
-        forward(ups_a, ups_v[:1])
+        forward(extra_w, only=later_rows & (side == 0))
+        forward(ups_a, only=jnp.logical_not(relays))
+        forward(ups_v, only=relays & jnp.logical_not(early))
         core = far * stacked(
             split(lower[...].T), split(jnp.concatenate([up_u[0], up_u[1]], axis=1))
         )
@@ -402,12 +424,11 @@
         wide[0] = both[:, :width]
         wide[1] = both[:, width:]
         begin(extra_w)
-        forward(ups_v[1:2])
         rank_1 = [ranks[1, 0, t, 0, r] for t in two]
         bases = [basis_of(here[t], above[t], u[t], wide[t], rank_1[t]) for t in two]
         bases = orthonormal(bases, rank_1, order_1, width)
-        forward(ups_v[2:])
-        forward(extra_w, only=later_rows)
+        forward(ups_v, only=middle)
+        forward(extra_w, only=later_rows & (side == 1))
         orthos = orthonormal(bases, rank_1, order_1, width)
         root_order = math.sqrt(height)
         tile_col = [t * n_col + c for t in two]
@@ -418,6 +439,7 @@
         for t in two:
             u1[t] = jnp.where(chosen[t], pad_rows(orthos[t] * root_order, width).T, u[t])
         begin(lows1_u)
+        forward(ups_v, only=jnp.logical_not(relays | middle))
         for t in two:
             right = new_right(backward(orthos[t], u[t], wide[t]), v[t], up_v[t]) * (1.0 / root_order)
             v1[t] = jnp.where(chosen[t], right, jnp.where(tile_col[t] == 0, lower[...], v[t]))
@@ -428,10 +450,8 @@
 
         @pl.when(r == 1)
         def _():
-            for t in two:
-                stays = tile_col[t] != 1
-                out_u[t] = jnp.where(stays, u1[t], 0.0)
-                out_v[t] = jnp.where(stays, v1[t], 0.0)
+            out_u[...] = u1[...]
+            out_v[...] = v1[...]
 
         @pl.when(later_rows)
         def _():
@@ -447,7 +467,9 @@
                 low1_own[...] = lower[...].T[:rows_1]
 
             begin(lows1_t)
-            forward(chains_u, lows1_u, chains_a, lows1_t)
+            forward(chains_u, chains_a)
+            forward(chains_v, only=spine)
+            forward(lows1_u, lows1_t)
             core = far * stacked(split(low1_t[...]), split(up1t[...].reshape(2 * width, height)), 1)
             both = deep(split(low1_u[...]), split(pad_rows(core, width)))
             wide[0] = both[:, :width]
@@ -455,9 +477,8 @@
             rank_2 = [ranks[2, 0, t, 0, r] for t in two]
             bases = [basis_of(here[t], above1[t], u1[t], wide[t], rank_2[t]) for t in two]
             bases = orthonormal(bases, rank_2, order_2, width)
-            forward(chains_v[:2])
             orthos = orthonormal(bases, rank_2, order_2, width)
-            forward(chains_v[2:])
+            forward(chains_v, only=jnp.logical_not(spine))
             for t in two:
                 live = tile_col[t] > 1
                 right = new_right(backward(orthos[t], u1[t], wide[t]), v1[t], up1_v[t]) * (1.0 / root_order)
@@ -484,7 +505,7 @@
     buffers += [f32(*s) for s in (one, one, one, one, pair, pair, (2, rows_1, width), (2, rows_1, width))]
     buffers += [f32(*s) for s in (one, one, one, pair, one, pair, pair, (2, rows_1, height), (2, rows_2, width))]
     buffers += [f32(*s) for s in ((2, width, height), pair, (2, rows_2, width), one, (rows_1, height), (rows_1, height))]
-    pieces = 45
+    pieces = 58
     any_spec = pl.BlockSpec(memory_space=pl.ANY)
     out_u, out_v = pl.pallas_call(
         functools.partial(kernel, n_row, n_col, order_1, order_2),
@@ -501,6 +522,9 @@
             collective_id=0, has_side_effects=True, vmem_limit_bytes=60 * 1024 * 1024
         ),
     )(ranks, u, v, near_field, sketch)
+    tile_col = jnp.arange(tiles, dtype=jnp.int32) * n_col + lax.axis_index("col")
+    stays = jnp.logical_not((lax.axis_index("row") == 1) & (tile_col == 1))[:, None, None]
+    out_u, out_v = jnp.where(stays, out_u, 0.0), jnp.where(stays, out_v, 0.0)
     shape_out = (1, 1, tiles, 1, height, width)
     return (out_u.reshape(shape_out), out_v.reshape(shape_out))
 

time: 89.4 us -> 78.4 us (0.88)
  Pallas kernels: 84.8 us -> 75.2 us
  local copies, waits for them, and re-layouts: 3.74 us -> 0 us
  other arithmetic: 0 us -> 2.31 us
    pallas_call x1, Pallas kernels: 84.8 us -> 75.2 us  [body(): pl.pallas_call(functools.partial(kernel, n_row, n_col, order_1, order_2),...]
    unnamed x2 -> x0, local copies, waits for them, and re-layouts: 3.74 us -> none
    unnamed x0 -> x1, other arithmetic: none -> 2.3 us
where the time goes in v2:
time: 78.4 us; the launch traced here: 78.2 us
  Pallas kernels  75.2 us (96%)
  other arithmetic  2.31 us (3%)
    pallas_call x1, Pallas kernels, body(): pl.pallas_call(functools.partial(kernel, n_row, n_col, order_1, order_2),...  75.2 us
    unnamed x1, other arithmetic  2.3 us

profile of v2, /device:TPU:30, one launch (start us, length us, event | category | flops | bytes accessed | tf_op | source)
XLA Modules:
  0.0 78.2 jit_solution(11500086170489388643)
XLA Ops:
  0.6 75.2 %shard_map.68 = (f32[2,512,128]{2,1,0:T(8,128)}, f32[2,512,128]{2,1,0:T(8,128)}) custom-call(s32[3,1,2,1,8]{4,3,2,1,0:T(1,128)} %bitcast.13, f32[2,512,128]{2,1,0:T(8,128)} %bitcast.11, f32[2,512,128]{2,1,0:T(8,128)} %bitcast.12, f32[2,512,512]{2,1,0:T(8,128)} %hnear.1, f32[2,512,128]{2,1,0:T(8,128)} %hsketch.1), custom_call_target="tpu_custom_call" | custom-call | tf_op jit(solution)/shard_map/pallas_call | solution.py:510
  75.9 2.3 %select_bitcast_fusion = (f32[1,1,2,1,512,128]{5,4,3,2,1,0:T(8,128)}, f32[1,1,2,1,512,128]{5,4,3,2,1,0:T(8,128)}) fusion(f32[2,512,128]{2,1,0:T(8,128)} %get-tuple-element.5, pred[2]{0:T(512)(128)(4,1)S(1)} %and_not_fusion, f32[2,512,128]{2,1,0:T(8,128)} %get-tuple-element.4), kind=kLoop, calls=%fused_computation | loop fusion | flops 262144 | bytes 2097154
  (1 shorter events, 0.0 us)

commit v3 on v2

--- a/solution.py
+++ b/solution.py
@@ -381,20 +381,25 @@
         last = level + 1 == levels
         relays = later_rows & jnp.logical_not(last) & (spine | ((level == 1) & (parity == 0)))
         ends = later_rows & jnp.logical_not(relays)
-        middle = ((r == 1) & (parity == 1)) | (last & spine)
+        odd = parity == 1
+        prompt = relays & (parity == 0)
+        middle = (odd & ((r == 1) | relays)) | (last & spine & (parity == 0))
+        late = jnp.logical_not(prompt | middle)
+        first_on = spine & jnp.logical_not(last) & ((level == 1) | (c != 1))
+        soon = first_on & odd & (level == 1)
         passes = relays | ((r == 1) & (parity == 1))
         leads = lambda cond: [forward(ups_u[t], only=passes & (parity != t) & cond) for t in two]
         forward(extras, only=later_rows & (side == 0))
         leads(c >= 2)
+        forward(lows_v, only=parity == 0)
         for k in two:
             forward(pivots[k], only=parity == k)
         leads(c < 2)
-        for t in two:
-            forward(ups_u[t], only=relays & (parity == t))
-        forward(ups_a, only=relays)
+        forward(lows_u, only=parity == 0)
+        forward(ups_u[0], ups_a, only=relays & (parity == 0))
         early = relays & (level == 1) & (parity == 0)
         forward(ups_v, only=early)
-        forward(lows_v, lows_u)
+        forward(lows_v, only=odd)
         for k in two:
             forward(pivots[k], only=parity != k)
         pivot_t = near_t[0] + far * deep(split(p_v[...]), split(p_u[...]), 1)
@@ -404,7 +409,7 @@
                 if k < 4:
                     forward(ups_u[t][k : k + 1], only=ends & (parity != t))
                 else:
-                    forward(ups_u[t][k - 4 : k - 3], only=(ends | ((r == 1) & (parity == 1))) & (parity == t))
+                    forward(ups_u[t][k - 4 : k - 3], only=(ends | odd) & (parity == t))
 
         hooks = {k: functools.partial(hook, k) for k in range(7)}
         lower[...] = apply_inverse(high, low, scale, low_v[...], hooks)
@@ -412,8 +417,9 @@
         forward(ups_u[1], ups_u[0], only=(r == 1) & (parity == 0))
         forward(extras, only=later_rows & (side == 1))
         forward(extra_w, only=later_rows & (side == 0))
-        forward(ups_a, only=jnp.logical_not(relays))
-        forward(ups_v, only=relays & jnp.logical_not(early))
+        forward(lows_u, only=odd)
+        forward(ups_a, only=odd | jnp.logical_not(relays))
+        forward(ups_v, only=prompt & jnp.logical_not(early))
         core = far * stacked(
             split(lower[...].T), split(jnp.concatenate([up_u[0], up_u[1]], axis=1))
         )
@@ -428,6 +434,7 @@
         bases = [basis_of(here[t], above[t], u[t], wide[t], rank_1[t]) for t in two]
         bases = orthonormal(bases, rank_1, order_1, width)
         forward(ups_v, only=middle)
+        forward(chains_u, only=later_rows & soon)
         forward(extra_w, only=later_rows & (side == 1))
         orthos = orthonormal(bases, rank_1, order_1, width)
         root_order = math.sqrt(height)
@@ -439,10 +446,30 @@
         for t in two:
             u1[t] = jnp.where(chosen[t], pad_rows(orthos[t] * root_order, width).T, u[t])
         begin(lows1_u)
-        forward(ups_v, only=jnp.logical_not(relays | middle))
-        for t in two:
+        forward(chains_u, only=later_rows & first_on & jnp.logical_not(soon))
+
+        def right_of(t):
             right = new_right(backward(orthos[t], u[t], wide[t]), v[t], up_v[t]) * (1.0 / root_order)
-            v1[t] = jnp.where(chosen[t], right, jnp.where(tile_col[t] == 0, lower[...], v[t]))
+            return jnp.where(chosen[t], right, jnp.where(tile_col[t] == 0, lower[...], v[t]))
+
+        forward(ups_v[:4], only=late)
+        v1[0] = right_of(0)
+
+        @pl.when((c == 1) & later_rows)
+        def _():
+            left = jnp.concatenate([ex_v[...], up_v[0]], axis=1)
+            right = jnp.concatenate([ex_u[...], -ex_w[...]], axis=1)
+            lh, ll = split(left)
+            rh, rl = split(right)
+            pivot_t = near_t[1] + far * (mm(lh, rh, 1) + (mm(lh, rl, 1) + mm(ll, rh, 1)))
+            high[...], low[...] = split(pivot_t)
+            lower[...] = apply_inverse(high, low, diagonal_inverse(near[1]), v1[0], {})
+            low1_own[...] = lower[...].T[:rows_1]
+
+        begin(lows1_t)
+        forward(lows1_u, only=later_rows & odd)
+        forward(ups_v[4:], only=late)
+        v1[1] = right_of(1)
         here = here_of(v1, 1)
         above1_own[0] = here[0]
         above1_own[1] = here[1]
@@ -455,21 +482,11 @@
 
         @pl.when(later_rows)
         def _():
-            @pl.when(c == 1)
-            def _():
-                left = jnp.concatenate([ex_v[...], up_v[0]], axis=1)
-                right = jnp.concatenate([ex_u[...], -ex_w[...]], axis=1)
-                lh, ll = split(left)
-                rh, rl = split(right)
-                pivot_t = near_t[1] + far * (mm(lh, rh, 1) + (mm(lh, rl, 1) + mm(ll, rh, 1)))
-                high[...], low[...] = split(pivot_t)
-                lower[...] = apply_inverse(high, low, diagonal_inverse(near[1]), v1[0], {})
-                low1_own[...] = lower[...].T[:rows_1]
-
-            begin(lows1_t)
-            forward(chains_u, chains_a)
-            forward(chains_v, only=spine)
-            forward(lows1_u, lows1_t)
+            forward(chains_u, only=jnp.logical_not(first_on))
+            forward(chains_a)
+            forward(lows1_t, only=odd)
+            forward(chains_v, only=spine & jnp.logical_not(last & odd))
+            forward(lows1_u, lows1_t, only=parity == 0)
             core = far * stacked(split(low1_t[...]), split(up1t[...].reshape(2 * width, height)), 1)
             both = deep(split(low1_u[...]), split(pad_rows(core, width)))
             wide[0] = both[:, :width]
@@ -477,6 +494,7 @@
             rank_2 = [ranks[2, 0, t, 0, r] for t in two]
             bases = [basis_of(here[t], above1[t], u1[t], wide[t], rank_2[t]) for t in two]
             bases = orthonormal(bases, rank_2, order_2, width)
+            forward(chains_v, only=spine & last & odd)
             orthos = orthonormal(bases, rank_2, order_2, width)
             forward(chains_v, only=jnp.logical_not(spine))
             for t in two:

time: 78.4 us -> 73.5 us (0.937)
  the two profiles are of different devices: /device:TPU:30 before, /device:TPU:28 now
where the time goes in v3:
time: 73.5 us; the launch traced here: 73.3 us
  Pallas kernels  70.4 us (96%)
  other arithmetic  2.31 us (3%)
    pallas_call x1, Pallas kernels, body(): pl.pallas_call(functools.partial(kernel, n_row, n_col, order_1, order_2),...  70.4 us
    unnamed x1, other arithmetic  2.3 us

profile of v3, /device:TPU:28, one launch (start us, length us, event | category | flops | bytes accessed | tf_op | source)
XLA Modules:
  0.0 73.3 jit_solution(9607619458842299219)
XLA Ops:
  0.6 70.4 %shard_map.68 = (f32[2,512,128]{2,1,0:T(8,128)}, f32[2,512,128]{2,1,0:T(8,128)}) custom-call(s32[3,1,2,1,8]{4,3,2,1,0:T(1,128)} %bitcast.13, f32[2,512,128]{2,1,0:T(8,128)} %bitcast.11, f32[2,512,128]{2,1,0:T(8,128)} %bitcast.12, f32[2,512,512]{2,1,0:T(8,128)} %hnear.1, f32[2,512,128]{2,1,0:T(8,128)} %hsketch.1), custom_call_target="tpu_custom_call" | custom-call | tf_op jit(solution)/shard_map/pallas_call | solution.py:528
  71.0 2.3 %select_bitcast_fusion = (f32[1,1,2,1,512,128]{5,4,3,2,1,0:T(8,128)}, f32[1,1,2,1,512,128]{5,4,3,2,1,0:T(8,128)}) fusion(f32[2,512,128]{2,1,0:T(8,128)} %get-tuple-element.5, pred[2]{0:T(512)(128)(4,1)S(1)} %and_not_fusion, f32[2,512,128]{2,1,0:T(8,128)} %get-tuple-element.4), kind=kLoop, calls=%fused_computation | loop fusion | flops 262144 | bytes 2097154
  (1 shorter events, 0.0 us)

commit v4 on v3

--- a/solution.py
+++ b/solution.py
@@ -409,16 +409,17 @@
                 if k < 4:
                     forward(ups_u[t][k : k + 1], only=ends & (parity != t))
                 else:
-                    forward(ups_u[t][k - 4 : k - 3], only=(ends | odd) & (parity == t))
+                    forward(ups_u[t][k - 4 : k - 3], only=ends & (parity == t))
+            if 0 < k < 5:
+                forward(ups_u[1][k - 1 : k], only=odd & jnp.logical_not(ends))
 
         hooks = {k: functools.partial(hook, k) for k in range(7)}
         lower[...] = apply_inverse(high, low, scale, low_v[...], hooks)
         hook(7)
         forward(ups_u[1], ups_u[0], only=(r == 1) & (parity == 0))
         forward(extras, only=later_rows & (side == 1))
-        forward(extra_w, only=later_rows & (side == 0))
+        forward(extra_w, only=later_rows & (side == 0) & jnp.logical_not(last))
         forward(lows_u, only=odd)
-        forward(ups_a, only=odd | jnp.logical_not(relays))
         forward(ups_v, only=prompt & jnp.logical_not(early))
         core = far * stacked(
             split(lower[...].T), split(jnp.concatenate([up_u[0], up_u[1]], axis=1))
@@ -430,12 +431,13 @@
         wide[0] = both[:, :width]
         wide[1] = both[:, width:]
         begin(extra_w)
+        forward(ups_a, only=odd | jnp.logical_not(relays))
         rank_1 = [ranks[1, 0, t, 0, r] for t in two]
         bases = [basis_of(here[t], above[t], u[t], wide[t], rank_1[t]) for t in two]
         bases = orthonormal(bases, rank_1, order_1, width)
         forward(ups_v, only=middle)
         forward(chains_u, only=later_rows & soon)
-        forward(extra_w, only=later_rows & (side == 1))
+        forward(extra_w, only=later_rows & (side == 0) & last)
         orthos = orthonormal(bases, rank_1, order_1, width)
         root_order = math.sqrt(height)
         tile_col = [t * n_col + c for t in two]
@@ -443,8 +445,12 @@
         for t in two:
             u1t_own[t] = orthos[t] * root_order
         begin(chains_u)
-        for t in two:
-            u1[t] = jnp.where(chosen[t], pad_rows(orthos[t] * root_order, width).T, u[t])
+
+        def set_left():
+            for t in two:
+                u1[t] = jnp.where(chosen[t], pad_rows(u1t_own[t], width).T, u[t])
+
+        pl.when(later_rows)(set_left)
         begin(lows1_u)
         forward(chains_u, only=later_rows & first_on & jnp.logical_not(soon))
 
@@ -457,6 +463,7 @@
 
         @pl.when((c == 1) & later_rows)
         def _():
+            forward(extra_w, only=side == 1)
             left = jnp.concatenate([ex_v[...], up_v[0]], axis=1)
             right = jnp.concatenate([ex_u[...], -ex_w[...]], axis=1)
             lh, ll = split(left)
@@ -467,7 +474,6 @@
             low1_own[...] = lower[...].T[:rows_1]
 
         begin(lows1_t)
-        forward(lows1_u, only=later_rows & odd)
         forward(ups_v[4:], only=late)
         v1[1] = right_of(1)
         here = here_of(v1, 1)
@@ -477,11 +483,13 @@
 
         @pl.when(r == 1)
         def _():
+            set_left()
             out_u[...] = u1[...]
             out_v[...] = v1[...]
 
         @pl.when(later_rows)
         def _():
+            forward(lows1_u, only=odd)
             forward(chains_u, only=jnp.logical_not(first_on))
             forward(chains_a)
             forward(lows1_t, only=odd)

time: 73.5 us -> 70.2 us (0.955)
  Pallas kernels: 70.4 us -> 67 us
    pallas_call x1, Pallas kernels: 70.4 us -> 67 us  [body(): pl.pallas_call(functools.partial(kernel, n_row, n_col, order_1, order_2),...]
where the time goes in v4:
time: 70.2 us; the launch traced here: 70 us
  Pallas kernels  67 us (95%)
  other arithmetic  2.31 us (3%)
    pallas_call x1, Pallas kernels, body(): pl.pallas_call(functools.partial(kernel, n_row, n_col, order_1, order_2),...  67 us
    unnamed x1, other arithmetic  2.3 us

profile of v4, /device:TPU:28, one launch (start us, length us, event | category | flops | bytes accessed | tf_op | source)
XLA Modules:
  0.0 70.0 jit_solution(11758566450853292841)
XLA Ops:
  0.6 67.0 %shard_map.68 = (f32[2,512,128]{2,1,0:T(8,128)}, f32[2,512,128]{2,1,0:T(8,128)}) custom-call(s32[3,1,2,1,8]{4,3,2,1,0:T(1,128)} %bitcast.13, f32[2,512,128]{2,1,0:T(8,128)} %bitcast.11, f32[2,512,128]{2,1,0:T(8,128)} %bitcast.12, f32[2,512,512]{2,1,0:T(8,128)} %hnear.1, f32[2,512,128]{2,1,0:T(8,128)} %hsketch.1), custom_call_target="tpu_custom_call" | custom-call | tf_op jit(solution)/shard_map/pallas_call | solution.py:536
  67.7 2.3 %select_bitcast_fusion = (f32[1,1,2,1,512,128]{5,4,3,2,1,0:T(8,128)}, f32[1,1,2,1,512,128]{5,4,3,2,1,0:T(8,128)}) fusion(f32[2,512,128]{2,1,0:T(8,128)} %get-tuple-element.5, pred[2]{0:T(512)(128)(4,1)S(1)} %and_not_fusion, f32[2,512,128]{2,1,0:T(8,128)} %get-tuple-element.4), kind=kLoop, calls=%fused_computation | loop fusion | flops 262144 | bytes 2097154
  (1 shorter events, 0.0 us)

commit v5 on v4

--- a/solution.py
+++ b/solution.py
@@ -535,7 +535,7 @@
     any_spec = pl.BlockSpec(memory_space=pl.ANY)
     out_u, out_v = pl.pallas_call(
         functools.partial(kernel, n_row, n_col, order_1, order_2),
-        out_shape=[jax.ShapeDtypeStruct(pair, F32)] * 2,
+        out_shape=[pltpu.VMEM(pair, F32)] * 2,
         in_specs=[pl.BlockSpec(memory_space=pltpu.SMEM)] + [any_spec] * 4,
         out_specs=[pl.BlockSpec(memory_space=pltpu.VMEM)] * 2,
         scratch_shapes=buffers

time: 70.2 us -> 68 us (0.969)
  other arithmetic: 2.31 us -> 1.11 us
  Pallas kernels: 67 us -> 66.1 us
    unnamed x1, other arithmetic: 2.3 us -> 1.1 us
    pallas_call x1, Pallas kernels: 67 us -> 66.1 us  [body(): pl.pallas_call(functools.partial(kernel, n_row, n_col, order_1, order_2),...]
where the time goes in v5:
time: 68 us; the launch traced here: 67.8 us
  Pallas kernels  66.1 us (97%)
  other arithmetic  1.11 us (2%)
    pallas_call x1, Pallas kernels, body(): pl.pallas_call(functools.partial(kernel, n_row, n_col, order_1, order_2),...  66.1 us

profile of v5, /device:TPU:28, one launch (start us, length us, event | category | flops | bytes accessed | tf_op | source)
XLA Modules:
  0.0 67.8 jit_solution(16006555263987432300)
XLA Ops:
  0.6 66.1 %shard_map.68 = (f32[2,512,128]{2,1,0:T(8,128)S(1)}, f32[2,512,128]{2,1,0:T(8,128)S(1)}) custom-call(s32[3,1,2,1,8]{4,3,2,1,0:T(1,128)} %bitcast.13, f32[2,512,128]{2,1,0:T(8,128)} %bitcast.11, f32[2,512,128]{2,1,0:T(8,128)} %bitcast.12, f32[2,512,512]{2,1,0:T(8,128)} %hnear.1, f32[2,512,128]{2,1,0:T(8,128)} %hsketch.1), custom_call_target="tpu_custom_call" | custom-call | tf_op jit(solution)/shard_map/pallas_call | solution.py:536
  66.7 1.1 %select_bitcast_fusion = (f32[1,1,2,1,512,128]{5,4,3,2,1,0:T(8,128)}, f32[1,1,2,1,512,128]{5,4,3,2,1,0:T(8,128)}) fusion(f32[2,512,128]{2,1,0:T(8,128)S(1)} %get-tuple-element.5, pred[2]{0:T(512)(128)(4,1)S(1)} %and_not_fusion, f32[2,512,128]{2,1,0:T(8,128)S(1)} %get-tuple-element.4), kind=kLoop, calls=%fused_computation | loop fusion | flops 262144 | bytes 2097154
  (1 shorter events, 0.0 us)

commit v6 on v5

--- a/solution.py
+++ b/solution.py
@@ -293,7 +293,7 @@
     lows_v = [across(part(v, 0, h, 2), part(low_v, None, h, 2), 0, r > 0) for h in two]
     lows_u = [across(part(u, 0, h, 2), part(low_u, None, h, 2), 0, r > 0) for h in two]
     ups_u = [[down(part(u, t, h, 4), part(up_u, t, h, 4), c > 0 if t == 0 else always, beside if t else [down_first]) for h in quarters] for t in two]
-    ups_a = [down(above_own, above, always, [down_first])]
+    ups_a = [down(above_own.at[t], above.at[t], always, [down_first]) for t in two]
     ups_v = [down(part(v, t, h, 4), part(up_v, t, h, 4), c > 0 if t == 0 else always, beside) for t in two for h in quarters]
     extras = [down_1(part(a, 0, h, 4), part(b, None, h, 4), 0, c == 1) for a, b in ((u, ex_u), (v, ex_v)) for h in quarters]
     extra_w = [down_1(part(wide, 0, h, 4), part(ex_w, None, h, 4), 0, c == 1) for h in quarters]
@@ -302,8 +302,8 @@
         for t in two
         for h in quarters
     ]
-    chains_a = [down_1(above1_own, above1, parity, always)]
-    chains_v = [down_1(part(v1, t, h, 2), part(up1_v, t, h, 2), parity, c > 1 if t == 0 else always) for t in two for h in two]
+    chains_a = [down_1(above1_own.at[t], above1.at[t], parity, always) for t in two]
+    chains_v = [down_1(part(v1, t, h, 4), part(up1_v, t, h, 4), parity, c > 1 if t == 0 else always) for t in two for h in quarters]
     lows1_u = [across(part(u1, 0, h, 2), part(low1_u, None, h, 2), 1, later_rows) for h in two]
     lows1_t = [across(part(low1_own, None, h, 2), part(low1_t, None, h, 2), 1, later_rows) for h in two]
 
@@ -460,6 +460,7 @@
 
         forward(ups_v[:4], only=late)
         v1[0] = right_of(0)
+        forward(ups_v[4:], only=late & spine)
 
         @pl.when((c == 1) & later_rows)
         def _():
@@ -474,7 +475,7 @@
             low1_own[...] = lower[...].T[:rows_1]
 
         begin(lows1_t)
-        forward(ups_v[4:], only=late)
+        forward(ups_v[4:], only=late & jnp.logical_not(spine))
         v1[1] = right_of(1)
         here = here_of(v1, 1)
         above1_own[0] = here[0]
@@ -531,7 +532,7 @@
     buffers += [f32(*s) for s in (one, one, one, one, pair, pair, (2, rows_1, width), (2, rows_1, width))]
     buffers += [f32(*s) for s in (one, one, one, pair, one, pair, pair, (2, rows_1, height), (2, rows_2, width))]
     buffers += [f32(*s) for s in ((2, width, height), pair, (2, rows_2, width), one, (rows_1, height), (rows_1, height))]
-    pieces = 58
+    pieces = 64
     any_spec = pl.BlockSpec(memory_space=pl.ANY)
     out_u, out_v = pl.pallas_call(
         functools.partial(kernel, n_row, n_col, order_1, order_2),

time: 68 us -> 67.7 us (level); the launches traced: 67.8 us -> 66.6 us
  Pallas kernels: 66.1 us -> 64.9 us
    pallas_call x1, Pallas kernels: 66.1 us -> 64.9 us  [body(): pl.pallas_call(functools.partial(kernel, n_row, n_col, order_1, order_2),...]
where the time goes in v6:
time: 67.7 us; the launch traced here: 66.6 us
  Pallas kernels  64.9 us (96%)
  other arithmetic  1.11 us (2%)
    pallas_call x1, Pallas kernels, body(): pl.pallas_call(functools.partial(kernel, n_row, n_col, order_1, order_2),...  64.9 us

profile of v6, /device:TPU:28, one launch (start us, length us, event | category | flops | bytes accessed | tf_op | source)
XLA Modules:
  0.0 66.6 jit_solution(2089832526367656044)
XLA Ops:
  0.6 64.9 %shard_map.68 = (f32[2,512,128]{2,1,0:T(8,128)S(1)}, f32[2,512,128]{2,1,0:T(8,128)S(1)}) custom-call(s32[3,1,2,1,8]{4,3,2,1,0:T(1,128)} %bitcast.13, f32[2,512,128]{2,1,0:T(8,128)} %bitcast.11, f32[2,512,128]{2,1,0:T(8,128)} %bitcast.12, f32[2,512,512]{2,1,0:T(8,128)} %hnear.1, f32[2,512,128]{2,1,0:T(8,128)} %hsketch.1), custom_call_target="tpu_custom_call" | custom-call | tf_op jit(solution)/shard_map/pallas_call | solution.py:537
  65.5 1.1 %select_bitcast_fusion = (f32[1,1,2,1,512,128]{5,4,3,2,1,0:T(8,128)}, f32[1,1,2,1,512,128]{5,4,3,2,1,0:T(8,128)}) fusion(f32[2,512,128]{2,1,0:T(8,128)S(1)} %get-tuple-element.5, pred[2]{0:T(512)(128)(4,1)S(1)} %and_not_fusion, f32[2,512,128]{2,1,0:T(8,128)S(1)} %get-tuple-element.4), kind=kLoop, calls=%fused_computation | loop fusion | flops 262144 | bytes 2097154
  (1 shorter events, 0.0 us)

commit v7 on v6

--- a/solution.py
+++ b/solution.py
@@ -493,8 +493,10 @@
             forward(lows1_u, only=odd)
             forward(chains_u, only=jnp.logical_not(first_on))
             forward(chains_a)
+            nearest = spine & jnp.logical_not(last) & odd & (level == 1)
+            forward(chains_v, only=nearest)
             forward(lows1_t, only=odd)
-            forward(chains_v, only=spine & jnp.logical_not(last & odd))
+            forward(chains_v, only=spine & jnp.logical_not((last & odd) | nearest))
             forward(lows1_u, lows1_t, only=parity == 0)
             core = far * stacked(split(low1_t[...]), split(up1t[...].reshape(2 * width, height)), 1)
             both = deep(split(low1_u[...]), split(pad_rows(core, width)))

time: 67.7 us -> 67.7 us (level)
  no operation moved by 1% of the time
where the time goes in v7:
time: 67.7 us; the launch traced here: 66.6 us
  Pallas kernels  64.9 us (96%)
  other arithmetic  1.11 us (2%)
    pallas_call x1, Pallas kernels, body(): pl.pallas_call(functools.partial(kernel, n_row, n_col, order_1, order_2),...  64.9 us

profile of v7, /device:TPU:28, one launch (start us, length us, event | category | flops | bytes accessed | tf_op | source)
XLA Modules:
  0.0 66.6 jit_solution(3420399419417296042)
XLA Ops:
  0.6 64.9 %shard_map.68 = (f32[2,512,128]{2,1,0:T(8,128)S(1)}, f32[2,512,128]{2,1,0:T(8,128)S(1)}) custom-call(s32[3,1,2,1,8]{4,3,2,1,0:T(1,128)} %bitcast.13, f32[2,512,128]{2,1,0:T(8,128)} %bitcast.11, f32[2,512,128]{2,1,0:T(8,128)} %bitcast.12, f32[2,512,512]{2,1,0:T(8,128)} %hnear.1, f32[2,512,128]{2,1,0:T(8,128)} %hsketch.1), custom_call_target="tpu_custom_call" | custom-call | tf_op jit(solution)/shard_map/pallas_call | solution.py:539
  65.5 1.1 %select_bitcast_fusion = (f32[1,1,2,1,512,128]{5,4,3,2,1,0:T(8,128)}, f32[1,1,2,1,512,128]{5,4,3,2,1,0:T(8,128)}) fusion(f32[2,512,128]{2,1,0:T(8,128)S(1)} %get-tuple-element.5, pred[2]{0:T(512)(128)(4,1)S(1)} %and_not_fusion, f32[2,512,128]{2,1,0:T(8,128)S(1)} %get-tuple-element.4), kind=kLoop, calls=%fused_computation | loop fusion | flops 262144 | bytes 2097154
  (1 shorter events, 0.0 us)
